TPU v7x, 32 devices: a whole 2x2x4 slice. The times are simulated.
32 devices in a mesh: kpt: 2 (over x), row: 8 (over z, y), col: 2 (over core).
Axes of the slice: x: 2, y: 2, z: 4, core: 2. Of those that a mesh axis runs over, the one named last changes fastest.
Arguments:
- wannier: float32 [64, 32, 1024], P('kpt', ('row', 'col')), parts along dimension 0, may hold values from -6 to 6
- pairs: int32 [384, 2], replicated, may hold values from 0 to 31, as said below
- gmap: int32 [8192], replicated, may hold values from 1 to 32767, as said below
- screened: bfloat16 [4, 2, 8192, 8192], P('kpt', None, 'row', 'col'), parts along dimension 0, may hold values from -0.046875 to 0.046875
Outputs:
- coulomb: float32 [2, 2, 768, 384], P(None, None, ('kpt', 'row', 'col')), parts along dimension 2
There are 2 independent parts, one for each index of `kpt`. A program takes and returns all parts, laid end to end along the dimension named above; an argument that names none is the same for every part. Nothing has to cross between parts.
Inputs may be any that keep to these rules, and one draw needn't show every extreme that they name: `gmap`: 8192 distinct flat cells of the grid; cell 0 is never among them. `pairs`: in each row the first Wannier function is no greater than the second; no two rows are equal.
All inputs are finite; a program needn't handle non-finite values.
Results may differ from a plain program's by a relative error of at most 0.0082.
Values may be sent and summed in bfloat16 or wider, within the bound.
No kernel may reach another device: no remote copies, remote signals or barrier semaphores. Data moves between devices by JAX's collectives and lax.ppermute only.
A program may use at most 128 MiB of HBM per device.

v0:
```python
import math
import jax
import jax.numpy as jnp
from jax import lax
from jax.sharding import PartitionSpec as P

NW = 32
GX = 32
NG = 8192
NP = 384


def line_tables(side_len):
    positions = jnp.arange(side_len, dtype=jnp.int32)
    phase_index = positions[:, None] * positions[None, :] % side_len
    angles = phase_index.astype(jnp.float32) * (2.0 * math.pi / side_len)
    return (jnp.cos(angles), jnp.sin(angles))


def plane_transform(density):
    cosine, sine_table = line_tables(GX)
    highest = lax.Precision.HIGHEST
    shaped = density.reshape(-1, GX, GX)
    real_z = jnp.einsum("nyz,kz->nyk", shaped, cosine, precision=highest)
    imag_z = -jnp.einsum("nyz,kz->nyk", shaped, sine_table, precision=highest)
    new_real = jnp.einsum("jy,nyk->njk", cosine, real_z, precision=highest) + jnp.einsum(
        "jy,nyk->njk", sine_table, imag_z, precision=highest
    )
    new_imag = jnp.einsum("jy,nyk->njk", cosine, imag_z, precision=highest) - jnp.einsum(
        "jy,nyk->njk", sine_table, real_z, precision=highest
    )
    return (new_real.reshape(density.shape), new_imag.reshape(density.shape))


def line_transform(real_part, imag_part):
    cosine, sine_table = line_tables(GX)
    highest = lax.Precision.HIGHEST
    new_real = jnp.einsum("kn,pny->pky", cosine, real_part, precision=highest) + jnp.einsum(
        "kn,pny->pky", sine_table, imag_part, precision=highest
    )
    new_imag = jnp.einsum("kn,pny->pky", cosine, imag_part, precision=highest) - jnp.einsum(
        "kn,pny->pky", sine_table, real_part, precision=highest
    )
    return (new_real, new_imag)


def right_columns(screened, segment):
    w_real = screened[:, 0]
    w_imag = screened[:, 1]
    real_real = jnp.einsum("fgh,bh->fgb", w_real, segment[0], preferred_element_type=jnp.float32)
    imag_imag = jnp.einsum("fgh,bh->fgb", w_imag, segment[1], preferred_element_type=jnp.float32)
    real_imag = jnp.einsum("fgh,bh->fgb", w_real, segment[1], preferred_element_type=jnp.float32)
    imag_real = jnp.einsum("fgh,bh->fgb", w_imag, segment[0], preferred_element_type=jnp.float32)
    return jnp.stack([real_real - imag_imag, real_imag + imag_real], axis=1)


def shards(wannier, pairs, gmap, screened):
    planes = wannier.shape[1]
    grid_cells = wannier.shape[2]
    members = jnp.arange(NW, dtype=jnp.int32)[None, :]
    pick_first = (pairs[:, 0:1] == members).astype(jnp.float32)
    pick_second = (pairs[:, 1:2] == members).astype(jnp.float32)
    flat_rows = wannier.reshape(NW, -1)
    highest = lax.Precision.HIGHEST
    density = jnp.dot(pick_first, flat_rows, precision=highest) * jnp.dot(
        pick_second, flat_rows, precision=highest
    )
    density = density.reshape(NP, planes, grid_cells)
    arrived = lax.all_to_all(density, ("row", "col"), split_axis=0, concat_axis=1, tiled=True)
    real_part, imag_part = plane_transform(arrived)
    real_part, imag_part = line_transform(real_part, imag_part)
    owned = real_part.shape[0]
    norm_factor = 1.0 / math.sqrt(GX * GX * GX)
    rho_real = jnp.take(real_part.reshape(owned, -1), gmap, axis=1) * norm_factor
    rho_imag = jnp.take(imag_part.reshape(owned, -1), gmap, axis=1) * norm_factor
    rho = jnp.stack([rho_real, rho_imag], axis=0).astype(jnp.bfloat16)
    row_span = screened.shape[2]
    halves = lax.all_to_all(rho, "col", split_axis=2, concat_axis=1, tiled=True)
    screened_rho = right_columns(screened, lax.all_gather(halves, "row", axis=1, tiled=True))
    blocks = lax.all_to_all(rho, "row", split_axis=2, concat_axis=1, tiled=True)
    blocks = blocks.reshape(2, lax.axis_size("row"), owned, row_span)
    left_panel = lax.all_gather(blocks, "col", axis=2, tiled=True).reshape(2, NP, row_span)
    left_wide = left_panel.astype(jnp.float32)
    u_real = jnp.einsum(
        "ag,fgb->fab", left_wide[0], screened_rho[:, 0], precision=highest
    ) + jnp.einsum("ag,fgb->fab", left_wide[1], screened_rho[:, 1], precision=highest)
    u_imag = jnp.einsum(
        "ag,fgb->fab", left_wide[0], screened_rho[:, 1], precision=highest
    ) - jnp.einsum("ag,fgb->fab", left_wide[1], screened_rho[:, 0], precision=highest)
    partial_terms = jnp.stack([u_real, u_imag], axis=1) / math.sqrt(NG)
    summed = lax.psum(partial_terms, ("row", "col"))
    share_rows = NP // lax.axis_size(("row", "col"))
    return lax.dynamic_slice_in_dim(
        summed, lax.axis_index(("row", "col")) * share_rows, share_rows, 2
    )


def solution(mesh):
    return jax.shard_map(
        shards,
        mesh=mesh,
        in_specs=(P("kpt", ("row", "col"), None), P(), P(), P("kpt", None, "row", "col")),
        out_specs=P(None, None, ("kpt", "row", "col"), None),
        check_vma=False,
    )
```

profile of v0, /device:TPU:0, one launch (start us, length us, event | category | flops | bytes accessed | tf_op | source)
XLA Modules:
  0.0 687.3 jit_solution(8600309741713015094)
XLA Ops:
  6.5 0.8 slice_reduce_fusion
  7.3 1.0 copy.93
  8.3 1.4 fusion.54
  9.8 1.5 convolution_multiply_fusion
  11.3 3.8 reshape.35
  15.1 7.5 %all-to-all-start = ((f32[384,2,1024]{2,1,0:T(2,128)}), f32[384,2,1024]{2,1,0:T(2,128)S(1)}, u32[]{:S(2)}, u32[]{:S(2)}) async-start(f32[384,2,1024]{2,1,0:T(2,128)} %reshape.35), calls=%async_computation | async-start | bytes 6291456 | tf_op jit(solution)/shard_map/all_to_all | solution.py:69
  22.6 0.0 all-gather.5.cloned.1.call-start
  22.7 0.0 copy-done.4
  22.7 59.1 %all-to-all-done = f32[384,2,1024]{2,1,0:T(2,128)S(1)} async-done(((f32[384,2,1024]{2,1,0:T(2,128)}), f32[384,2,1024]{2,1,0:T(2,128)S(1)}, u32[]{:S(2)}, u32[]{:S(2)}) %all-to-all-start) | async-done | bytes 3145760 | tf_op jit(solution)/shard_map/all_to_all | solution.py:69
  81.9 1.0 copy.70
  82.9 2.4 copy.71
  85.3 7.6 %reshape.36 = f32[768,32,32]{2,1,0:T(8,128)} reshape(f32[24,16,2,1024]{3,2,1,0:T(2,128)S(1)} %copy.71) | data formatting | bytes 6291456 | tf_op jit(solution)/shard_map/reshape | solution.py:23
  92.9 9.2 %copy.72 = f32[768,32,32]{0,2,1:T(8,128)S(1)} copy(f32[768,32,32]{2,1,0:T(8,128)} %reshape.36) | data formatting | bytes 6291456 | tf_op jit(solution)/shard_map/reshape | solution.py:23
  102.1 3.0 convolution_negate_fusion
  105.1 3.0 fusion.72
  108.1 4.9 fusion.22
  113.1 5.2 fusion.24
  118.2 6.7 add_bitcast_fusion.1
  125.0 5.5 subtract_bitcast_fusion.1
  130.5 10.6 %copy.79 = f32[768,32,32]{2,1,0:T(8,128)} copy(f32[768,32,32]{0,1,2:T(8,128)S(1)} %subtract_bitcast_fusion.1) | data formatting | bytes 6291456 | tf_op jit(solution)/shard_map/sub | solution.py:29
  141.1 9.4 %reshape.38 = f32[24,32,1024]{2,1,0:T(8,128)S(1)} reshape(f32[768,32,32]{2,1,0:T(8,128)} %copy.79) | data formatting | bytes 6291456 | tf_op jit(solution)/shard_map/reshape | solution.py:32
  150.4 5.5 fusion.66
  155.9 11.4 %copy.76 = f32[768,32,32]{2,1,0:T(8,128)} copy(f32[768,32,32]{0,1,2:T(8,128)} %add_bitcast_fusion.1) | data formatting | bytes 6291456 | tf_op jit(solution)/shard_map/add | solution.py:26
  167.3 10.7 %reshape.37 = f32[24,32,1024]{2,1,0:T(8,128)} reshape(f32[768,32,32]{2,1,0:T(8,128)} %copy.76) | data formatting | bytes 6291456 | tf_op jit(solution)/shard_map/reshape | solution.py:32
  178.0 5.9 fusion.69
  184.0 5.5 subtract_bitcast_fusion
  189.5 5.6 add_bitcast_fusion
  195.1 10.3 %copy.89 = f32[24,32,1024]{0,2,1:T(8,128)} copy(f32[24,32,1024]{2,1,0:T(8,128)} %add_bitcast_fusion) | data formatting | bytes 6291456 | tf_op jit(solution)/shard_map/reshape | solution.py:74
  205.4 0.0 copy-done.2
  205.4 8.6 %copy.90 = f32[24,32,1024]{0,2,1:T(8,128)} copy(f32[24,32,1024]{2,1,0:T(8,128)S(1)} %copy-done.2) | data formatting | bytes 6291456 | tf_op jit(solution)/shard_map/reshape | solution.py:75
  214.0 33.6 %gather_fusion = f32[8192,24]{1,0:T(8,128)} fusion(f32[24,32768]{0,1:T(8,128)} %bitcast.144, s32[8192]{0:T(1024)S(1)} %fusion.57), kind=kCustom, calls=%fused_computation.clone | custom fusion | bytes 1605632 | tf_op jit(solution)/shard_map/jit(_take)/gather | solution.py:74
  247.6 33.6 %gather_fusion.1 = f32[8192,24]{1,0:T(8,128)} fusion(f32[24,32768]{0,1:T(8,128)} %bitcast.143, s32[8192]{0:T(1024)S(1)} %fusion.57), kind=kCustom, calls=%fused_computation.1.clone | custom fusion | bytes 1605632 | tf_op jit(solution)/shard_map/jit(_take)/gather | solution.py:75
  281.3 7.2 %fusion.30 = (bf16[1,24,8192]{1,2,0:T(8,128)(2,1)S(1)}, bf16[1,24,8192]{1,2,0:T(8,128)(2,1)S(1)}) fusion(f32[8192,24]{1,0:T(8,128)} %gather_fusion, pred[8192]{0:T(1024)(128)(4,1)S(1)} %compare_and_fusion, f32[8192,24]{1,0:T(8,128)} %gather_fusion.1), kind=kLoop, calls=%fused_computation.43 | loop fusion | flops 1179648 | bytes 2367488 | tf_op jit(solution)/shard_map/stack | solution.py:76
  288.4 0.9 pad_maximum_fusion
  289.4 35.5 %copy.108 = bf16[2,24,8192]{1,0,2:T(2,128)(2,1)} copy(bf16[2,24,8192]{1,2,0:T(8,128)(2,1)S(1)} %pad_maximum_fusion) | data formatting | bytes 1572864 | tf_op jit(solution)/shard_map/stack | solution.py:76
  324.9 6.6 reshape.71
  331.5 35.8 %all_to_all.48 = bf16[8,2,24576]{2,1,0:T(2,128)(2,1)S(1)} all-to-all(bf16[8,2,24576]{2,1,0:T(2,128)(2,1)S(1)} %reshape.71), channel_id=1, replica_groups=mesh['kpt'=2,'row'=8,'col'=2] {'row'}, dimensions={0} | all-to-all | bytes 1572864 | tf_op jit(solution)/shard_map/all_to_all | solution.py:80
  367.3 6.9 %reshape.72 = bf16[8192,2,24]{2,1,0:T(2,128)(2,1)} reshape(bf16[8,2,24576]{2,1,0:T(2,128)(2,1)S(1)} %all_to_all.48) | data formatting | bytes 1572864
  374.3 10.3 %copy.87 = bf16[2,24,8,1024]{3,1,2,0:T(8,128)(2,1)} copy(bf16[2,24,8,1024]{1,0,3,2:T(2,128)(2,1)} %bitcast.145) | data formatting | bytes 1572864 | tf_op jit(solution)/shard_map/all_to_all | solution.py:80
  384.6 0.0 all-gather.5.cloned.1.call-update
  384.6 0.0 all-gather.3.cloned.1.call-start
  384.6 10.2 %copy.109 = bf16[2,24,8192]{1,0,2:T(2,128)(2,1)} copy(bf16[2,24,8192]{1,2,0:T(8,128)(2,1)} %copy-done) | data formatting | bytes 1572864 | tf_op jit(solution)/shard_map/stack | solution.py:76
  394.8 7.0 %reshape.73 = bf16[2,2,98304]{2,1,0:T(2,128)(2,1)S(1)} reshape(bf16[8192,2,24]{2,1,0:T(2,128)(2,1)} %bitcast.147) | data formatting | bytes 1572864
  401.9 4.4 all_to_all.49
  406.2 7.3 %reshape.74 = bf16[8192,2,24]{2,1,0:T(2,128)(2,1)} reshape(bf16[2,2,98304]{2,1,0:T(2,128)(2,1)S(1)} %all_to_all.49) | data formatting | bytes 1572864
  413.6 9.5 %copy.83 = bf16[2,24,2,4096]{3,1,2,0:T(8,128)(2,1)} copy(bf16[2,24,2,4096]{1,0,3,2:T(2,128)(2,1)} %bitcast.146) | data formatting | bytes 1572864 | tf_op jit(solution)/shard_map/all_to_all | solution.py:78
  423.0 0.0 all-gather.3.cloned.1.call-update
  423.1 0.0 all-reduce.2.cloned.1.call-start
  423.1 0.0 all-gather.5.cloned.1.call-done
  423.1 1.5 fusion.129
  424.7 96.3 %all-gather.3.cloned.1.call-done = bf16[2,384,4096]{2,1,0:T(8,128)(2,1)} async-done(((bf16[2,48,4096]{2,1,0:T(8,128)(2,1)}), bf16[2,384,4096]{2,1,0:T(8,128)(2,1)}) %all-gather.3.cloned.1.call-update) | async-done | bytes 6291472 | tf_op jit(solution)/shard_map/all_gather | solution.py:79
  521.0 11.4 %fusion = f32[384,2,1024]{2,0,1:T(8,128)S(1)} fusion(bf16[2,2,1024,4096]{3,2,1,0:T(8,128)(2,1)} %param.9, bf16[2,384,4096]{2,1,0:T(8,128)(2,1)} %all-gather.3.cloned.1.call-done), kind=kOutput, calls=%fused_computation.2 | convolution fusion | flops 6442450944 | bytes 23068672 | tf_op jit(solution)/shard_map/fgh,bh->fgb/dot_general | solution.py:53
  532.4 11.2 %fusion.39 = f32[384,2,1024]{2,0,1:T(8,128)S(1)} fusion(f32[384,2,1024]{2,0,1:T(8,128)S(1)} %fusion, bf16[2,2,1024,4096]{3,2,1,0:T(8,128)(2,1)} %param.9, bf16[2,384,4096]{2,1,0:T(8,128)(2,1)} %all-gather.3.cloned.1.call-done), kind=kOutput, calls=%fused_computation.47 | convolution fusion | flops 6443237376 | bytes 26214400 | tf_op jit(solution)/shard_map/fgh,bh->fgb/dot_general | solution.py:52
  543.6 2.6 fusion.14
  546.2 2.6 fusion.16
  548.9 12.6 %fusion.2 = f32[384,2,1024]{2,0,1:T(8,128)} fusion(bf16[2,2,1024,4096]{3,2,1,0:T(8,128)(2,1)} %param.9, bf16[2,384,4096]{2,1,0:T(8,128)(2,1)} %all-gather.3.cloned.1.call-done), kind=kOutput, calls=%fused_computation.4 | convolution fusion | flops 6442450944 | bytes 23068672 | tf_op jit(solution)/shard_map/fgh,bh->fgb/dot_general | solution.py:51
  561.5 12.1 %fusion.36 = f32[384,2,1024]{2,0,1:T(8,128)S(1)} fusion(f32[384,2,1024]{2,0,1:T(8,128)} %fusion.2, bf16[2,2,1024,4096]{3,2,1,0:T(8,128)(2,1)} %param.9, bf16[2,384,4096]{2,1,0:T(8,128)(2,1)} %all-gather.3.cloned.1.call-done), kind=kOutput, calls=%fused_computation.46 | convolution fusion | flops 6443237376 | bytes 26214400 | tf_op jit(solution)/shard_map/fgh,bh->fgb/dot_general | solution.py:50
  573.6 2.7 fusion.48
  576.3 2.7 fusion.51
  579.0 1.6 maximum_multiply_fusion
  580.6 0.0 all-reduce.2.cloned.1.call-update
  580.6 97.4 %all-reduce.2.cloned.1.call-done = f32[2,2,384,384]{2,3,0,1:T(8,128)} async-done(((f32[2,2,384,384]{2,3,0,1:T(8,128)}), f32[2,2,384,384]{2,3,0,1:T(8,128)}) %all-reduce.2.cloned.1.call-update) | async-done | bytes 2359312 | tf_op jit(solution)/shard_map/psum | solution.py:91
  678.0 1.7 constant_dynamic-slice_fusion
  679.6 0.9 copy.88
  (10 shorter events, 0.0 us)
Async XLA Ops:
  15.1 7.6 %copy-start.4 = (s32[8192]{0:T(1024)S(1)}, s32[8192]{0:T(1024)}, u32[]{:S(2)}) copy-start(s32[8192]{0:T(1024)} %param.8) | copy-start | bytes 98308
  15.1 66.8 %all-to-all-start = ((f32[384,2,1024]{2,1,0:T(2,128)}), f32[384,2,1024]{2,1,0:T(2,128)S(1)}, u32[]{:S(2)}, u32[]{:S(2)}) async-start(f32[384,2,1024]{2,1,0:T(2,128)} %reshape.35), calls=%async_computation | async-start | bytes 6291456 | tf_op jit(solution)/shard_map/all_to_all | solution.py:69
  22.6 400.5 %all-gather.5.cloned.1.call-start = ((), (), s32[]{:S(2)}) async-start(), calls=%async_computation.4 | async-start | bytes 2359296 | tf_op jit(solution)/shard_map/all_gather | solution.py:82
  178.0 6.0 copy-start.1
  178.0 6.0 copy-start.3
  195.1 10.3 %copy-start.2 = (f32[24,32,1024]{2,1,0:T(8,128)S(1)}, f32[24,32,1024]{2,1,0:T(8,128)}, u32[]{:S(2)}) copy-start(f32[24,32,1024]{2,1,0:T(8,128)} %subtract_bitcast_fusion) | copy-start | bytes 9437188
  289.4 35.5 %copy-start = (bf16[2,24,8192]{1,2,0:T(8,128)(2,1)}, bf16[2,24,8192]{1,2,0:T(8,128)(2,1)S(1)}, u32[]{:S(2)}) copy-start(bf16[2,24,8192]{1,2,0:T(8,128)(2,1)S(1)} %pad_maximum_fusion) | copy-start | bytes 2359300
  384.6 136.4 %all-gather.3.cloned.1.call-start = ((), (), s32[]{:S(2)}) async-start(), calls=%async_computation.3 | async-start | bytes 7077888 | tf_op jit(solution)/shard_map/all_gather | solution.py:79
  423.1 254.9 %all-reduce.2.cloned.1.call-start = ((), (), s32[]{:S(2)}) async-start(), calls=%async_computation.5 | async-start | bytes 4718592 | tf_op jit(solution)/shard_map/psum | solution.py:91
Sparse Core Ops, SparseCore 0:
  384.7 8.8 all-gather.4
  423.2 97.7 all-gather.2
  580.7 97.1 all-reduce.1
where the time goes:
time: 696 us; the launch traced here: 687 us
  waiting for transfers between devices  253 us (36%)
  local copies, waits for them, and re-layouts  251 us (36%)
  matrix products  112 us (16%)
  blocking collectives  40.2 us (6%)
  between operations  13.7 us (2%)
  other arithmetic  9.75 us (1%)
  starting transfers between devices  7.67 us (1%)
    psum x1, waiting for transfers between devices, shards(): summed = lax.psum(partial_terms, ('row', 'col'))  97.4 us
    all_gather x1, waiting for transfers between devices, shards(): lax.all_gather(halves, 'row', axis=1, tiled=True)  96.3 us
    all_to_all x1, waiting for transfers between devices, shards(): lax.all_to_all(density, ('row', 'col'), split_axis=0, concat_axis=1, tile...  59.1 us
    another operation x2, local copies, waits for them, and re-layouts, shards(): rho = jnp.stack([rho_real, rho_imag], axis=0).astype(jnp.bfloat16)  45.7 us
    all_to_all x1, blocking collectives, shards(): blocks = lax.all_to_all(rho, 'row', split_axis=2, concat_axis=1, tiled=True)  35.8 us
    gather x1, local copies, waits for them, and re-layouts, shards(): jnp.take(imag_part.reshape(owned, -1), gmap, axis=1) * norm_factor  33.6 us
    gather x1, local copies, waits for them, and re-layouts, shards(): jnp.take(real_part.reshape(owned, -1), gmap, axis=1) * norm_factor  33.6 us
    unnamed x15, local copies, waits for them, and re-layouts  29 us
  transfers between devices with their start and end apart: 4, of which 3 were waited for; matrix products, arithmetic and copies ran while one was open for 5% of the time, Pallas kernels for 0%

commit v1 on v0

--- a/solution.py
+++ b/solution.py
@@ -8,6 +8,7 @@
 GX = 32
 NG = 8192
 NP = 384
+spot_post = lambda mine: lax.psum(lax.psum(mine, axis_name="row"), axis_name="col")
 
 
 def line_tables(side_len):
@@ -88,7 +89,7 @@
         "ag,fgb->fab", left_wide[0], screened_rho[:, 1], precision=highest
     ) - jnp.einsum("ag,fgb->fab", left_wide[1], screened_rho[:, 0], precision=highest)
     partial_terms = jnp.stack([u_real, u_imag], axis=1) / math.sqrt(NG)
-    summed = lax.psum(partial_terms, ("row", "col"))
+    summed = spot_post(partial_terms)
     share_rows = NP // lax.axis_size(("row", "col"))
     return lax.dynamic_slice_in_dim(
         summed, lax.axis_index(("row", "col")) * share_rows, share_rows, 2

time: 696 us -> 728 us (1.046)
  waiting for transfers between devices: 253 us -> 285 us
    psum x1 -> x2, waiting for transfers between devices: 97.4 us -> 130 us  [the longest x1 107 us: lax.psum(mine, axis_name='row')]
  transfers between devices with their start and end apart: 4 -> 5, of which waited for: 3 -> 4; matrix products, arithmetic and copies ran while one was open for 5% -> 5% of each run, Pallas kernels for 0% -> 0%
where the time goes in v1:
time: 728 us; the launch traced here: 720 us
  waiting for transfers between devices  285 us (39%)
  local copies, waits for them, and re-layouts  251 us (34%)
  matrix products  112 us (15%)
  blocking collectives  40.2 us (6%)
  between operations  13.6 us (2%)
  other arithmetic  9.75 us (1%)
  starting transfers between devices  7.71 us (1%)
    psum x1, waiting for transfers between devices, lax.psum(mine, axis_name='row')  107 us
    all_gather x1, waiting for transfers between devices, shards(): lax.all_gather(halves, 'row', axis=1, tiled=True)  96.3 us
    all_to_all x1, waiting for transfers between devices, shards(): lax.all_to_all(density, ('row', 'col'), split_axis=0, concat_axis=1, tile...  59.1 us
    another operation x2, local copies, waits for them, and re-layouts, shards(): rho = jnp.stack([rho_real, rho_imag], axis=0).astype(jnp.bfloat16)  45.7 us
    all_to_all x1, blocking collectives, shards(): blocks = lax.all_to_all(rho, 'row', split_axis=2, concat_axis=1, tiled=True)  35.8 us
    gather x1, local copies, waits for them, and re-layouts, shards(): jnp.take(imag_part.reshape(owned, -1), gmap, axis=1) * norm_factor  33.6 us
    gather x1, local copies, waits for them, and re-layouts, shards(): jnp.take(real_part.reshape(owned, -1), gmap, axis=1) * norm_factor  33.6 us
    unnamed x15, local copies, waits for them, and re-layouts  29 us
  transfers between devices with their start and end apart: 5, of which 4 were waited for; matrix products, arithmetic and copies ran while one was open for 5% of the time, Pallas kernels for 0%

profile of v1, /device:TPU:0, one launch (start us, length us, event | category | flops | bytes accessed | tf_op | source)
XLA Modules:
  0.0 719.8 jit_solution(13501091259790191071)
XLA Ops:
  6.5 0.8 slice_reduce_fusion
  7.3 1.0 copy.93
  8.3 1.4 fusion.54
  9.8 1.5 convolution_multiply_fusion
  11.3 3.8 reshape.35
  15.1 7.5 %all-to-all-start = ((f32[384,2,1024]{2,1,0:T(2,128)}), f32[384,2,1024]{2,1,0:T(2,128)S(1)}, u32[]{:S(2)}, u32[]{:S(2)}) async-start(f32[384,2,1024]{2,1,0:T(2,128)} %reshape.35), calls=%async_computation | async-start | bytes 6291456 | tf_op jit(solution)/shard_map/all_to_all | solution.py:70
  22.6 0.0 all-gather.5.cloned.1.call-start
  22.7 59.1 %all-to-all-done = f32[384,2,1024]{2,1,0:T(2,128)S(1)} async-done(((f32[384,2,1024]{2,1,0:T(2,128)}), f32[384,2,1024]{2,1,0:T(2,128)S(1)}, u32[]{:S(2)}, u32[]{:S(2)}) %all-to-all-start) | async-done | bytes 3145760 | tf_op jit(solution)/shard_map/all_to_all | solution.py:70
  81.9 1.0 copy.70
  82.9 2.4 copy.71
  85.3 7.6 %reshape.36 = f32[768,32,32]{2,1,0:T(8,128)} reshape(f32[24,16,2,1024]{3,2,1,0:T(2,128)S(1)} %copy.71) | data formatting | bytes 6291456 | tf_op jit(solution)/shard_map/reshape | solution.py:24
  92.9 9.2 %copy.72 = f32[768,32,32]{0,2,1:T(8,128)S(1)} copy(f32[768,32,32]{2,1,0:T(8,128)} %reshape.36) | data formatting | bytes 6291456 | tf_op jit(solution)/shard_map/reshape | solution.py:24
  102.1 3.0 convolution_negate_fusion
  105.1 3.0 fusion.72
  108.1 4.9 fusion.22
  113.1 5.2 fusion.24
  118.2 6.7 add_bitcast_fusion.1
  125.0 5.5 subtract_bitcast_fusion.1
  130.5 10.6 %copy.79 = f32[768,32,32]{2,1,0:T(8,128)} copy(f32[768,32,32]{0,1,2:T(8,128)S(1)} %subtract_bitcast_fusion.1) | data formatting | bytes 6291456 | tf_op jit(solution)/shard_map/sub | solution.py:30
  141.1 9.4 %reshape.38 = f32[24,32,1024]{2,1,0:T(8,128)S(1)} reshape(f32[768,32,32]{2,1,0:T(8,128)} %copy.79) | data formatting | bytes 6291456 | tf_op jit(solution)/shard_map/reshape | solution.py:33
  150.4 5.5 fusion.66
  155.9 11.4 %copy.76 = f32[768,32,32]{2,1,0:T(8,128)} copy(f32[768,32,32]{0,1,2:T(8,128)} %add_bitcast_fusion.1) | data formatting | bytes 6291456 | tf_op jit(solution)/shard_map/add | solution.py:27
  167.3 10.7 %reshape.37 = f32[24,32,1024]{2,1,0:T(8,128)} reshape(f32[768,32,32]{2,1,0:T(8,128)} %copy.76) | data formatting | bytes 6291456 | tf_op jit(solution)/shard_map/reshape | solution.py:33
  178.0 5.9 fusion.69
  184.0 5.5 subtract_bitcast_fusion
  189.5 5.6 add_bitcast_fusion
  195.1 10.3 %copy.89 = f32[24,32,1024]{0,2,1:T(8,128)} copy(f32[24,32,1024]{2,1,0:T(8,128)} %add_bitcast_fusion) | data formatting | bytes 6291456 | tf_op jit(solution)/shard_map/reshape | solution.py:75
  205.4 8.6 %copy.90 = f32[24,32,1024]{0,2,1:T(8,128)} copy(f32[24,32,1024]{2,1,0:T(8,128)S(1)} %copy-done.2) | data formatting | bytes 6291456 | tf_op jit(solution)/shard_map/reshape | solution.py:76
  214.0 33.6 %gather_fusion = f32[8192,24]{1,0:T(8,128)} fusion(f32[24,32768]{0,1:T(8,128)} %bitcast.144, s32[8192]{0:T(1024)S(1)} %fusion.57), kind=kCustom, calls=%fused_computation.clone | custom fusion | bytes 1605632 | tf_op jit(solution)/shard_map/jit(_take)/gather | solution.py:75
  247.6 33.6 %gather_fusion.1 = f32[8192,24]{1,0:T(8,128)} fusion(f32[24,32768]{0,1:T(8,128)} %bitcast.143, s32[8192]{0:T(1024)S(1)} %fusion.57), kind=kCustom, calls=%fused_computation.1.clone | custom fusion | bytes 1605632 | tf_op jit(solution)/shard_map/jit(_take)/gather | solution.py:76
  281.3 7.2 fusion.30
  288.4 0.9 pad_maximum_fusion
  289.4 35.5 %copy.108 = bf16[2,24,8192]{1,0,2:T(2,128)(2,1)} copy(bf16[2,24,8192]{1,2,0:T(8,128)(2,1)S(1)} %pad_maximum_fusion) | data formatting | bytes 1572864 | tf_op jit(solution)/shard_map/stack | solution.py:77
  324.9 6.6 reshape.71
  331.5 35.8 %all_to_all.48 = bf16[8,2,24576]{2,1,0:T(2,128)(2,1)S(1)} all-to-all(bf16[8,2,24576]{2,1,0:T(2,128)(2,1)S(1)} %reshape.71), channel_id=1, replica_groups=mesh['kpt'=2,'row'=8,'col'=2] {'row'}, dimensions={0} | all-to-all | bytes 1572864 | tf_op jit(solution)/shard_map/all_to_all | solution.py:81
  367.3 6.9 reshape.72
  374.3 10.3 %copy.87 = bf16[2,24,8,1024]{3,1,2,0:T(8,128)(2,1)} copy(bf16[2,24,8,1024]{1,0,3,2:T(2,128)(2,1)} %bitcast.145) | data formatting | bytes 1572864 | tf_op jit(solution)/shard_map/all_to_all | solution.py:81
  384.6 0.0 all-gather.5.cloned.1.call-update
  384.6 0.0 all-gather.3.cloned.1.call-start
  384.6 10.2 %copy.109 = bf16[2,24,8192]{1,0,2:T(2,128)(2,1)} copy(bf16[2,24,8192]{1,2,0:T(8,128)(2,1)} %copy-done) | data formatting | bytes 1572864 | tf_op jit(solution)/shard_map/stack | solution.py:77
  394.8 7.0 reshape.73
  401.9 4.4 all_to_all.49
  406.2 7.3 %reshape.74 = bf16[8192,2,24]{2,1,0:T(2,128)(2,1)} reshape(bf16[2,2,98304]{2,1,0:T(2,128)(2,1)S(1)} %all_to_all.49) | data formatting | bytes 1572864
  413.6 9.5 %copy.83 = bf16[2,24,2,4096]{3,1,2,0:T(8,128)(2,1)} copy(bf16[2,24,2,4096]{1,0,3,2:T(2,128)(2,1)} %bitcast.146) | data formatting | bytes 1572864 | tf_op jit(solution)/shard_map/all_to_all | solution.py:79
  423.0 0.0 all-gather.3.cloned.1.call-update
  423.1 0.0 all-reduce.3.cloned.1.call-start
  423.1 0.0 all-gather.5.cloned.1.call-done
  423.1 1.5 fusion.129
  424.7 96.3 %all-gather.3.cloned.1.call-done = bf16[2,384,4096]{2,1,0:T(8,128)(2,1)} async-done(((bf16[2,48,4096]{2,1,0:T(8,128)(2,1)}), bf16[2,384,4096]{2,1,0:T(8,128)(2,1)}) %all-gather.3.cloned.1.call-update) | async-done | bytes 6291472 | tf_op jit(solution)/shard_map/all_gather | solution.py:80
  521.0 11.4 %fusion = f32[384,2,1024]{2,0,1:T(8,128)S(1)} fusion(bf16[2,2,1024,4096]{3,2,1,0:T(8,128)(2,1)} %param.9, bf16[2,384,4096]{2,1,0:T(8,128)(2,1)} %all-gather.3.cloned.1.call-done), kind=kOutput, calls=%fused_computation.2 | convolution fusion | flops 6442450944 | bytes 23068672 | tf_op jit(solution)/shard_map/fgh,bh->fgb/dot_general | solution.py:54
  532.3 11.2 %fusion.39 = f32[384,2,1024]{2,0,1:T(8,128)S(1)} fusion(f32[384,2,1024]{2,0,1:T(8,128)S(1)} %fusion, bf16[2,2,1024,4096]{3,2,1,0:T(8,128)(2,1)} %param.9, bf16[2,384,4096]{2,1,0:T(8,128)(2,1)} %all-gather.3.cloned.1.call-done), kind=kOutput, calls=%fused_computation.47 | convolution fusion | flops 6443237376 | bytes 26214400 | tf_op jit(solution)/shard_map/fgh,bh->fgb/dot_general | solution.py:53
  543.6 2.6 fusion.14
  546.2 2.6 fusion.16
  548.9 12.6 %fusion.2 = f32[384,2,1024]{2,0,1:T(8,128)} fusion(bf16[2,2,1024,4096]{3,2,1,0:T(8,128)(2,1)} %param.9, bf16[2,384,4096]{2,1,0:T(8,128)(2,1)} %all-gather.3.cloned.1.call-done), kind=kOutput, calls=%fused_computation.4 | convolution fusion | flops 6442450944 | bytes 23068672 | tf_op jit(solution)/shard_map/fgh,bh->fgb/dot_general | solution.py:52
  561.5 11.9 %fusion.36 = f32[384,2,1024]{2,0,1:T(8,128)S(1)} fusion(f32[384,2,1024]{2,0,1:T(8,128)} %fusion.2, bf16[2,2,1024,4096]{3,2,1,0:T(8,128)(2,1)} %param.9, bf16[2,384,4096]{2,1,0:T(8,128)(2,1)} %all-gather.3.cloned.1.call-done), kind=kOutput, calls=%fused_computation.46 | convolution fusion | flops 6443237376 | bytes 26214400 | tf_op jit(solution)/shard_map/fgh,bh->fgb/dot_general | solution.py:51
  573.3 2.7 fusion.48
  576.0 2.7 fusion.51
  578.7 1.6 maximum_multiply_fusion
  580.3 0.0 all-reduce.5.cloned.1.call-start
  580.4 106.9 %all-reduce.3.cloned.1.call-done = f32[2,2,384,384]{2,3,0,1:T(8,128)} async-done(((f32[2,2,384,384]{2,3,0,1:T(8,128)}), f32[2,2,384,384]{2,3,0,1:T(8,128)}) %all-reduce.3.cloned.1.call-update) | async-done | bytes 2359312 | tf_op jit(solution)/shard_map/psum | solution.py:11
  687.3 0.0 all-reduce.5.cloned.1.call-update
  687.3 23.1 %all-reduce.5.cloned.1.call-done = f32[2,2,384,384]{2,3,0,1:T(8,128)} async-done(((f32[2,2,384,384]{2,3,0,1:T(8,128)}), f32[2,2,384,384]{2,3,0,1:T(8,128)}) %all-reduce.5.cloned.1.call-update) | async-done | bytes 2359312 | tf_op jit(solution)/shard_map/psum | solution.py:11
  710.4 1.7 constant_dynamic-slice_fusion
  712.1 0.9 copy.88
  (13 shorter events, 0.1 us)
Async XLA Ops:
  15.1 7.6 %copy-start.4 = (s32[8192]{0:T(1024)S(1)}, s32[8192]{0:T(1024)}, u32[]{:S(2)}) copy-start(s32[8192]{0:T(1024)} %param.8) | copy-start | bytes 98308
  15.1 66.8 %all-to-all-start = ((f32[384,2,1024]{2,1,0:T(2,128)}), f32[384,2,1024]{2,1,0:T(2,128)S(1)}, u32[]{:S(2)}, u32[]{:S(2)}) async-start(f32[384,2,1024]{2,1,0:T(2,128)} %reshape.35), calls=%async_computation | async-start | bytes 6291456 | tf_op jit(solution)/shard_map/all_to_all | solution.py:70
  22.6 400.5 %all-gather.5.cloned.1.call-start = ((), (), s32[]{:S(2)}) async-start(), calls=%async_computation.4 | async-start | bytes 2359296 | tf_op jit(solution)/shard_map/all_gather | solution.py:83
  178.0 6.0 copy-start.1
  178.0 6.0 copy-start.3
  195.1 10.3 %copy-start.2 = (f32[24,32,1024]{2,1,0:T(8,128)S(1)}, f32[24,32,1024]{2,1,0:T(8,128)}, u32[]{:S(2)}) copy-start(f32[24,32,1024]{2,1,0:T(8,128)} %subtract_bitcast_fusion) | copy-start | bytes 9437188
  289.4 35.5 %copy-start = (bf16[2,24,8192]{1,2,0:T(8,128)(2,1)}, bf16[2,24,8192]{1,2,0:T(8,128)(2,1)S(1)}, u32[]{:S(2)}) copy-start(bf16[2,24,8192]{1,2,0:T(8,128)(2,1)S(1)} %pad_maximum_fusion) | copy-start | bytes 2359300
  384.6 136.4 %all-gather.3.cloned.1.call-start = ((), (), s32[]{:S(2)}) async-start(), calls=%async_computation.3 | async-start | bytes 7077888 | tf_op jit(solution)/shard_map/all_gather | solution.py:80
  423.1 264.2 %all-reduce.3.cloned.1.call-start = ((), (), s32[]{:S(2)}) async-start(), calls=%async_computation.5 | async-start | bytes 4718592 | tf_op jit(solution)/shard_map/psum | solution.py:11
  580.3 130.1 %all-reduce.5.cloned.1.call-start = ((), (), s32[]{:S(2)}) async-start(), calls=%async_computation.6 | async-start | bytes 4718592 | tf_op jit(solution)/shard_map/psum | solution.py:11
Sparse Core Ops, SparseCore 0:
  384.7 8.8 all-gather.4
  423.2 97.7 all-gather.2
  580.5 106.7 all-reduce.2
  689.5 20.9 all-reduce.4
